TPU v7x, 512 devices: a 4x2x32 block of a 4x8x32 slice. The times are simulated.
512 devices in a mesh: groups: 2 (over y), seq: 32 (over z), head: 4 (over x), rep: 2 (over core).
Axes of the slice: x: 4, y: 2, z: 32, core: 2. Of those that a mesh axis runs over, the one named last changes fastest.
The devices are a block of a 4x8x32 slice.
Arguments:
- prefix_x: bfloat16 [8192, 8192], P(('groups', 'seq'), ('head', 'rep')), parts along dimension 0, may hold values from -6 to 6
- prefix_b: bfloat16 [8192, 8, 256], P(('groups', 'seq'), ('head', 'rep')), parts along dimension 0, may hold values from -0.09375 to 0.09375
- prefix_c: bfloat16 [8192, 8, 256], P(('groups', 'seq'), ('head', 'rep')), parts along dimension 0, may hold values from -0.375 to 0.375
- prefix_decay: float32 [8192, 128], P(('groups', 'seq'), ('head', 'rep')), parts along dimension 0, may hold values from 0 to 1.5, as said below
- bypass_weight: float32 [128], replicated, may hold values from 0.1 to 1.9
- prefix_key_rows: bfloat16 [8192, 4, 128], P(('groups', 'seq'), 'head'), parts along dimension 0, may hold values from -8 to 8
- prefix_values: bfloat16 [8192, 4, 128], P(('groups', 'seq'), 'head'), parts along dimension 0, may hold values from -6 to 6
- cand_x: bfloat16 [128, 32, 8192], P(('groups', 'seq', 'rep'), None, 'head'), parts along dimension 0, may hold values from -6 to 6
- cand_b: bfloat16 [128, 32, 8, 256], P(('groups', 'seq', 'rep'), None, 'head'), parts along dimension 0, may hold values from -0.09375 to 0.09375
- cand_c: bfloat16 [128, 32, 8, 256], P(('groups', 'seq', 'rep'), None, 'head'), parts along dimension 0, may hold values from -0.375 to 0.375
- cand_decay: float32 [128, 32, 128], P(('groups', 'seq', 'rep'), None, 'head'), parts along dimension 0, may hold values from 0 to 1.5, as said below
- cand_queries: bfloat16 [128, 32, 32, 128], P(('groups', 'seq', 'rep'), None, 'head'), parts along dimension 0, may hold values from -8 to 8
- cand_keys: bfloat16 [128, 32, 4, 128], P(('groups', 'seq', 'rep'), None, 'head'), parts along dimension 0, may hold values from -16 to 16
- cand_values: bfloat16 [128, 32, 4, 128], P(('groups', 'seq', 'rep'), None, 'head'), parts along dimension 0, may hold values from -6 to 6
- cand_length: int32 [128], P(('groups', 'seq', 'rep')), parts along dimension 0, may hold values from 16 to 32
Outputs:
- prefix_out: bfloat16 [8192, 8192], P(('groups', 'seq'), ('head', 'rep')), parts along dimension 0
- cand_ssm: bfloat16 [128, 32, 8192], P(('groups', 'seq', 'rep'), None, 'head'), parts along dimension 0
- cand_attn: bfloat16 [128, 32, 32, 128], P(('groups', 'seq', 'rep'), None, 'head'), parts along dimension 0
There are 2 independent parts, one for each index of `groups`. A program takes and returns all parts, laid end to end along the dimension named above; an argument that names none is the same for every part. Nothing has to cross between parts.
Inputs may be any that keep to these rules, and one draw needn't show every extreme that they name: `prefix_decay`: positive. `cand_decay`: positive.
All inputs are finite; a program needn't handle non-finite values.
Results may differ from a plain program's by a relative error of at most 0.008.
Values may be sent and summed in bfloat16 or wider, within the bound.
A program may use at most 128 MiB of HBM per device.

v0:
```python
import math
import jax
import jax.numpy as jnp
from jax import lax
from jax.sharding import PartitionSpec as P

EPSILON = 1e-06
FLOOR = -1e30


def entering(part, axis, combine, identity):
    place = lax.axis_index(axis)
    gathered = jax.tree.map(lambda a: lax.all_gather(a, axis), part)
    state = jax.tree.map(lambda a, e: jnp.zeros_like(a) + jnp.asarray(e, a.dtype), part, identity)

    def one(hop, state):
        return combine(
            state, jax.tree.map(lambda a: lax.dynamic_index_in_dim(a, hop, 0, False), gathered)
        )

    return lax.fori_loop(0, place, one, state)


def copy_for_each(x, axis):
    count = lax.axis_size(axis)
    return lax.all_to_all(jnp.broadcast_to(x[None], (count, *x.shape)), axis, 0, 0, tiled=True)


def combined_pairwise(pieces, combine):
    while len(jax.tree.leaves(pieces)[0]) > 1:
        pieces = jax.vmap(combine)(*(pieces[side::2] for side in (0, 1)))
    return pieces[0]


def entering_2(x, axis, combine, identity):
    count, position = (lax.axis_size(axis), lax.axis_index(axis))
    passed = jnp.arange(count) > position

    def kept(part, zero, own):
        part = jnp.where(
            passed.reshape(-1, *(1 for _ in own.shape)), part, jnp.asarray(zero, own.dtype)
        )
        return part[::-1]

    pieces = copy_for_each(x, axis)
    return combined_pairwise(kept(pieces, identity, x), combine)


def laid_out(tiles, dim):
    tiles = jnp.moveaxis(tiles, 0, dim)
    lengths = tiles.shape
    return tiles.reshape(*lengths[:dim], lengths[dim] * lengths[dim + 1], *lengths[dim + 2 :])


def gather_directly(x, axis, dim):
    return laid_out(copy_for_each(x, axis), dim)


def sent_together(arrays, axis, dim, along):
    widths = [a.shape[along] for a in arrays]
    both = jnp.concatenate(arrays, axis=along)
    result = lax.all_gather(both, axis, axis=dim, tiled=True)
    return tuple(jnp.split(result, [sum(widths[:k]) for k in range(1, len(widths))], axis=along))


def summarize(x, bmat, decay):
    length, groups, state = bmat.shape
    heads = decay.shape[1]
    per_group = heads // groups
    width = x.shape[1] // heads
    cum = jnp.cumsum(decay, axis=0)
    total = jnp.exp(-cum[-1])
    weights = jnp.exp(cum[-1][None, :] - cum)
    inputs = x.reshape(length, heads, width)
    weighted = (inputs.astype(jnp.float32) * weights[:, :, None]).astype(jnp.bfloat16)
    weighted = weighted.reshape(length, groups, per_group, width)
    local = jnp.einsum("sgn,sgkp->gknp", bmat, weighted, preferred_element_type=jnp.float32)
    return (cum, total, local.reshape(heads, state, width))


def emit(x, bmat, cmat, cum, skip, start):
    length, groups, state = bmat.shape
    heads = cum.shape[1]
    per_group = heads // groups
    width = x.shape[1] // heads
    inputs = x.reshape(length, heads, width)
    gram = jnp.einsum("tgn,sgn->gts", cmat, bmat, preferred_element_type=jnp.float32)
    span = math.gcd(per_group, 4)
    count = heads // span
    causal = lax.broadcasted_iota(jnp.int32, (length, length), 0) >= lax.broadcasted_iota(
        jnp.int32, (length, length), 1
    )
    cum_sets = cum.T.reshape(count, span, length)
    input_sets = inputs.reshape(length, count, span, width).transpose(1, 0, 2, 3)

    def one_set(piece):
        index, cum_set, input_set = piece
        gram_set = lax.dynamic_index_in_dim(gram, index * span // per_group, 0, keepdims=False)
        gap = cum_set[:, :, None] - cum_set[:, None, :]
        state_mixing = jnp.where(causal, jnp.exp(-jnp.where(causal, gap, 0.0)), 0.0) * gram_set
        return jnp.einsum(
            "hts,shp->thp",
            state_mixing.astype(jnp.bfloat16),
            input_set,
            preferred_element_type=jnp.float32,
        )

    intra = lax.map(one_set, (jnp.arange(count, dtype=jnp.int32), cum_sets, input_sets))
    intra = intra.transpose(1, 0, 2, 3).reshape(length, heads, width)
    start_set = start.reshape(groups, per_group, state, width)
    carried = jnp.einsum("tgn,gknp->tgkp", cmat.astype(jnp.float32), start_set)
    carried = carried.reshape(length, heads, width)
    result = (
        intra
        + jnp.exp(-cum)[:, :, None] * carried
        + skip[None, :, None] * inputs.astype(jnp.float32)
    )
    return result.reshape(length, heads * width).astype(jnp.bfloat16)


def chain_step(earlier, later):
    return (earlier[0] * later[0], later[0][:, None, None] * earlier[1] + later[1])


def elementwise_product(earlier, later):
    return earlier * later


def blend(carry, scores, values):
    top, mass, acc = carry
    new_top = jnp.maximum(top, scores.max(-1))
    fade = jnp.exp(top - new_top)
    weights = jnp.exp(scores - new_top[..., None])
    mass = mass * fade + weights.sum(-1)
    acc = acc * fade[..., None] + jnp.einsum(
        "ctkqs,skd->ctkqd", weights.astype(jnp.bfloat16), values, preferred_element_type=jnp.float32
    )
    return (new_top, mass, acc)


def join(first, second):
    top = jnp.maximum(first[0], second[0])
    one = jnp.exp(first[0] - top)
    two = jnp.exp(second[0] - top)
    return (
        top,
        first[1] * one + second[1] * two,
        first[2] * one[..., None] + second[2] * two[..., None],
    )


def key_folder(query_set, scale, carry, piece):
    keys, values = piece
    rows = keys.shape[0]
    step = math.gcd(rows, 1024)

    def one_block(inner, index):
        key_block = lax.dynamic_slice_in_dim(keys, index * step, step, 0)
        value_block = lax.dynamic_slice_in_dim(values, index * step, step, 0)
        scores = (
            jnp.einsum("ctkqd,skd->ctkqs", query_set, key_block, preferred_element_type=jnp.float32)
            * scale
        )
        return (blend(inner, scores, value_block), None)

    carry, unused = lax.scan(one_block, carry, jnp.arange(rows // step, dtype=jnp.int32))
    return carry


def empty_softmax(count, steps, kv_local, per_kv, dim):
    shape = (count, steps, kv_local, per_kv)
    return (
        jnp.full(shape, FLOOR, jnp.float32),
        jnp.zeros(shape, jnp.float32),
        jnp.zeros(shape + (dim,), jnp.float32),
    )


def on_device(
    prefix_x,
    prefix_b,
    prefix_c,
    prefix_decay,
    bypass_weight,
    prefix_key_rows,
    prefix_values,
    cand_x,
    cand_b,
    cand_c,
    cand_decay,
    cand_queries,
    cand_keys,
    cand_values,
    cand_length,
):
    local_heads = prefix_decay.shape[1]
    spread = lax.axis_size("rep")
    offset = (lax.axis_index("head") * spread + lax.axis_index("rep")) * local_heads
    skip_local = lax.dynamic_slice_in_dim(bypass_weight, offset, local_heads)
    cum, total, local = summarize(prefix_x, prefix_b, prefix_decay)
    identity = (jnp.ones_like(total), jnp.zeros_like(local))
    carried_in = entering((total, local), "seq", chain_step, identity)[1]
    prefix_out = emit(prefix_x, prefix_b, prefix_c, cum, skip_local, carried_in)
    beyond = entering_2(total, "seq", elementwise_product, jnp.ones_like(total))
    final = lax.psum(beyond[:, None, None] * local, "seq")
    heads_final = gather_directly(final, "rep", 0)
    cand_heads = cand_decay.shape[2]
    cand_skip = lax.dynamic_slice_in_dim(
        bypass_weight, lax.axis_index("head") * cand_heads, cand_heads
    )
    steps = cand_x.shape[1]
    valid = lax.broadcasted_iota(jnp.int32, (steps,), 0) < cand_length[0]
    cand_cum = jnp.cumsum(cand_decay[0], axis=0)
    cand_out = emit(cand_x[0], cand_b[0], cand_c[0], cand_cum, cand_skip, heads_final)
    cand_ssm = jnp.where(valid[:, None], cand_out, jnp.zeros((), jnp.bfloat16))[None]
    kv_local = prefix_key_rows.shape[1]
    dim = prefix_key_rows.shape[2]
    per_kv = cand_queries.shape[2] // kv_local
    scale = dim ** (-0.5)
    query = cand_queries[0].reshape(steps, kv_local, per_kv, dim)
    init = empty_softmax(1, steps, kv_local, per_kv, dim)
    part = key_folder(
        query[None], scale, init, sent_together((prefix_key_rows, prefix_values), "seq", 0, 1)
    )
    part = (part[0][0], part[1][0], part[2][0])
    own_scores = (
        jnp.einsum("tkqd,skd->tkqs", query, cand_keys[0], preferred_element_type=jnp.float32)
        * scale
    )
    visible = lax.broadcasted_iota(jnp.int32, (steps, 1, 1, steps), 0) >= lax.broadcasted_iota(
        jnp.int32, (steps, 1, 1, steps), 3
    )
    own_scores = jnp.where(visible, own_scores, FLOOR)
    own_top = own_scores.max(-1)
    own_weights = jnp.exp(own_scores - own_top[..., None])
    own_acc = jnp.einsum(
        "tkqs,skd->tkqd",
        own_weights.astype(jnp.bfloat16),
        cand_values[0],
        preferred_element_type=jnp.float32,
    )
    top, mass, acc = join(part, (own_top, own_weights.sum(-1), own_acc))
    mixed = acc / mass[..., None]
    mixed = mixed * lax.rsqrt(jnp.mean(mixed * mixed, axis=-1, keepdims=True) + EPSILON)
    mixed = mixed.reshape(steps, kv_local * per_kv, dim)
    cand_attn = jnp.where(valid[:, None, None], mixed, 0.0).astype(jnp.bfloat16)[None]
    return (prefix_out, cand_ssm, cand_attn)


def solution(mesh):
    placed = (
        P(("groups", "seq"), ("head", "rep")),
        P(("groups", "seq"), ("head", "rep"), None),
        P(("groups", "seq"), ("head", "rep"), None),
        P(("groups", "seq"), ("head", "rep")),
        P(),
        P(("groups", "seq"), "head", None),
        P(("groups", "seq"), "head", None),
        P(("groups", "seq", "rep"), None, "head"),
        P(("groups", "seq", "rep"), None, "head", None),
        P(("groups", "seq", "rep"), None, "head", None),
        P(("groups", "seq", "rep"), None, "head"),
        P(("groups", "seq", "rep"), None, "head", None),
        P(("groups", "seq", "rep"), None, "head", None),
        P(("groups", "seq", "rep"), None, "head", None),
        P(("groups", "seq", "rep")),
    )
    return jax.shard_map(
        on_device,
        mesh=mesh,
        in_specs=placed,
        out_specs=(
            P(("groups", "seq"), ("head", "rep")),
            P(("groups", "seq", "rep"), None, "head"),
            P(("groups", "seq", "rep"), None, "head", None),
        ),
        check_vma=False,
    )
```

profile of v0, /device:TPU:2016, one launch (start us, length us, event | category | flops | bytes accessed | tf_op | source)
XLA Modules:
  0.0 707.2 jit_solution(14934478910430227610)
XLA Ops:
  10.3 5.2 all-to-all-start
  16.9 17.7 %all-to-all-done = f32[32,1,16]{2,1,0:T(1,128)S(1)} async-done(((f32[32,1,16]{2,1,0:T(1,128)}), f32[32,1,16]{2,1,0:T(1,128)S(1)}, u32[]{:S(2)}, u32[]{:S(2)}) %all-to-all-start) | async-done | bytes 2080 | tf_op jit(solution)/shard_map/all_to_all | solution.py:26
  40.7 13.2 %while.56 = (s32[]{:T(128)}, f32[8,32,4,64]{3,1,2,0:T(8,128)S(1)}, bf16[8,32,4,64]{3,2,0,1:T(4,128)(2,1)S(1)}, f32[8,4,32]{2,1,0:T(4,128)S(1)}, s32[8]{0:T(128)S...) while((s32[]{:T(128)}, f32[8,32,4,64]{3,1,2,0:T(8,128)S(1)}, ...), condition=%wide.region_7.8_spmd.clone.clone, body=%wide.region_6.7_spmd.clone.clone.sunk | while | flops 549909 | bytes 166245 | solution.py:108
  54.7 53.0 %all-gather = f32[32,1,16]{2,1,0:T(1,128)S(1)} all-gather(f32[1,1,16]{2,1,0:T(1,128)S(1)} %get-tuple-element.433), channel_id=1, replica_groups=mesh['groups'=2,'seq'=32,'head'=4,'rep'=2] {'seq'}, dimensions={0}, use_global_device_ids=true | all-gather | bytes 2112 | tf_op jit(solution)/shard_map/all_gather | solution.py:13
  107.8 3.9 while.55
  111.7 133.8 %all-reduce.1 = bf16[16,256,64]{1,2,0:T(8,128)(2,1)S(1)} all-reduce(f32[16,256,64]{1,2,0:T(8,128)S(1)} %get-tuple-element.436), channel_id=1, replica_groups=mesh['groups'=2,'seq'=32,'head'=4,'rep'=2] {'seq'}, use_global_device_ids=true, to_apply=%region_8.9 | all-reduce | flops 262144 | bytes 1572864 | tf_op jit(solution)/shard_map/psum | solution.py:205
  245.6 4.6 all_to_all.14
  253.8 9.7 %while.57 = (s32[]{:T(128)}, f32[1,32,1,8]{1,3,2,0:T(8,128)S(1)}, f32[1,32,1,8]{1,3,2,0:T(8,128)S(1)}, f32[1,32,1,8,128]{4,1,3,0,2:T(8,128)S(1)}, s32[4]{0:T(128...) while((s32[]{:T(128)}, f32[1,32,1,8]{1,3,2,0:T(8,128)S(1)}, ...), condition=%wide.region_12.13_spmd.clone, body=%wide.region_9.12_spmd.clone.sunk | while | flops 135890432 | bytes 4020427 | solution.py:166
  264.8 251.0 %all-gather.4.cloned.1.call-done = f32[32,16,256,64]{2,3,1,0:T(8,128)} async-done(((f32[1,16,256,64]{2,3,1,0:T(8,128)}), f32[32,16,256,64]{2,3,1,0:T(8,128)}) %all-gather.4.cloned.1.call-update) | async-done | bytes 33554448 | tf_op jit(solution)/shard_map/all_gather | solution.py:13
  517.4 179.7 %while.54 = (s32[]{:T(128)}, f32[16,256,64]{2,1,0:T(8,128)}, s32[]{:T(128)}, f32[32,16]{1,0:T(8,128)S(1)}, f32[32,16,256,64]{2,3,1,0:T(8,128)}, /*index=5*/s32[]{:T(128)}, s32[]{:T(128)}, s32[]{:T(128)}) while((s32[]{:T(128)}, f32[16,256,64]{2,1,0:T(8,128)}, s32[]{:T(128)}, f32[32,16]{1,0:T(8,128)S(1)}, f32[32,16,256,64]{2,3,1,0:T(8,128)}, ...), condition=%wide.region_4.5_spmd, body=%wide.region_3.4_spmd.sunk | while | flops 524293 | bytes 7356799 | solution.py:21
  520.0 3.2 bitcast_add_fusion.4
  531.6 3.2 bitcast_add_fusion.4
  537.4 3.2 bitcast_add_fusion.4
  548.9 3.2 bitcast_add_fusion.4
  554.7 3.2 bitcast_add_fusion.4
  560.5 3.2 bitcast_add_fusion.4
  572.1 3.2 bitcast_add_fusion.4
  577.9 3.2 bitcast_add_fusion.4
  583.7 3.2 bitcast_add_fusion.4
  595.3 3.2 bitcast_add_fusion.4
  601.1 3.2 bitcast_add_fusion.4
  606.9 3.2 bitcast_add_fusion.4
  618.5 3.2 bitcast_add_fusion.4
  624.3 3.2 bitcast_add_fusion.4
  630.1 3.2 bitcast_add_fusion.4
  641.7 3.2 bitcast_add_fusion.4
  647.5 3.2 bitcast_add_fusion.4
  659.1 3.2 bitcast_add_fusion.4
  664.9 3.2 bitcast_add_fusion.4
  670.7 3.2 bitcast_add_fusion.4
  682.3 3.2 bitcast_add_fusion.4
  688.1 3.2 bitcast_add_fusion.4
  (422 shorter events, 146.1 us)
Async XLA Ops:
  7.2 27.8 %copy-start = (bf16[128,1,256]{2,0,1:T(8,128)(2,1)S(1)}, bf16[128,1,256]{2,0,1:T(8,128)(2,1)}, u32[]{:S(2)}) copy-start(bf16[128,1,256]{2,0,1:T(8,128)(2,1)} %param.24) | copy-start | bytes 196612
  7.2 244.9 %all-gather.6.cloned.1.call-start = ((), (), s32[]{:S(2)}) async-start(), calls=%async_computation.3 | async-start | bytes 2162688 | tf_op jit(solution)/shard_map/all_gather | solution.py:62
  10.3 24.3 %all-to-all-start = ((f32[32,1,16]{2,1,0:T(1,128)}), f32[32,1,16]{2,1,0:T(1,128)S(1)}, u32[]{:S(2)}, u32[]{:S(2)}) async-start(f32[32,1,16]{2,1,0:T(1,128)} %broadcast_in_dim.151), calls=%async_computation | async-start | bytes 32768 | tf_op jit(solution)/shard_map/all_to_all | solution.py:26
  15.5 500.4 %all-gather.4.cloned.1.call-start = ((), (), s32[]{:S(2)}) async-start(), calls=%async_computation.2 | async-start | bytes 34603008 | tf_op jit(solution)/shard_map/all_gather | solution.py:13
  16.8 20.1 %copy-start.15 = (f32[128]{0:T(128)S(1)}, f32[128]{0:T(128)}, u32[]{:S(2)}) copy-start(f32[128]{0:T(128)} %param.27) | copy-start | bytes 1540
  16.8 21.8 %copy-start.10 = (f32[1,32,32]{2,1,0:T(8,128)S(1)}, f32[1,32,32]{2,1,0:T(8,128)}, u32[]{:S(2)}) copy-start(f32[1,32,32]{2,1,0:T(8,128)} %param.33) | copy-start | bytes 12292
  16.9 21.9 %copy-start.3 = (bf16[1,32,8,128]{3,2,1,0:T(8,128)(2,1)S(1)}, bf16[1,32,8,128]{3,2,1,0:T(8,128)(2,1)}, u32[]{:S(2)}) copy-start(bf16[1,32,8,128]{3,2,1,0:T(8,128)(2,1)} %param.34) | copy-start | bytes 196612
  16.9 22.0 %copy-start.13 = (bf16[1,32,1,128]{3,1,2,0:T(8,128)(2,1)S(1)}, bf16[1,32,1,128]{3,1,2,0:T(8,128)(2,1)}, u32[]{:S(2)}) copy-start(bf16[1,32,1,128]{3,1,2,0:T(8,128)(2,1)} %param.35) | copy-start | bytes 24580
  34.9 5.0 copy-start.2
  36.2 4.4 copy-start.5
  36.2 4.4 copy-start.7
  40.6 67.1 %copy-start.4 = (bf16[128,1,256]{2,0,1:T(8,128)(2,1)S(1)}, bf16[128,1,256]{2,0,1:T(8,128)(2,1)}, u32[]{:S(2)}) copy-start(bf16[128,1,256]{2,0,1:T(8,128)(2,1)} %param.25) | copy-start | bytes 196612
  253.8 9.8 %copy-start.9 = (f32[32,8]{0,1:T(8,128)S(1)}, f32[32,8]{0,1:T(8,128)}, u32[]{:S(2)}) copy-start(f32[32,8]{0,1:T(8,128)} %get-tuple-element.429) | copy-start | bytes 3076
  253.8 10.0 %copy-start.14 = (bf16[1,32,1,128]{3,1,2,0:T(8,128)(2,1)S(1)}, bf16[1,32,1,128]{3,1,2,0:T(8,128)(2,1)}, u32[]{:S(2)}) copy-start(bf16[1,32,1,128]{3,1,2,0:T(8,128)(2,1)} %param.36) | copy-start | bytes 24580
  525.7 3.3 copy-start.12
  531.5 3.3 copy-start.12
  543.1 3.3 copy-start.12
  548.9 3.3 copy-start.12
  554.7 3.3 copy-start.12
  566.3 3.3 copy-start.12
  572.1 3.3 copy-start.12
  589.5 3.3 copy-start.12
  595.3 3.3 copy-start.12
  612.7 3.3 copy-start.12
  618.5 3.3 copy-start.12
  635.9 3.3 copy-start.12
  641.7 3.3 copy-start.12
  653.3 3.3 copy-start.12
  659.1 3.3 copy-start.12
  664.9 3.3 copy-start.12
  676.5 3.3 copy-start.12
  682.3 3.3 copy-start.12
  (47 other events, 66.5 us)
Sparse Core Ops, SparseCore 0:
  10.7 119.5 all-gather.5
  132.4 383.4 all-gather.3
where the time goes:
time: 710 us; the launch traced here: 707 us
  waiting for transfers between devices  269 us (38%)
  blocking collectives  191 us (27%)
  other arithmetic  106 us (15%)
  local copies, waits for them, and re-layouts  97.6 us (14%)
  between operations  15.1 us (2%)
  matrix products  13.4 us (2%)
  loops' own time  9.57 us (1%)
    all_gather x1, waiting for transfers between devices, entering(): gathered = jax.tree.map(lambda a: lax.all_gather(a, axis), part)  251 us
    psum x1, blocking collectives, on_device(): final = lax.psum(beyond[:, None, None] * local, 'seq')  134 us
    add x31, other arithmetic, chain_step(): later[0][:, None, None] * earlier[1] + later[1]  100 us
    dynamic_slice x62, local copies, waits for them, and re-layouts, one(): lax.dynamic_index_in_dim(a, hop, 0, False)  59.4 us
    all_gather x1, blocking collectives, entering(): gathered = jax.tree.map(lambda a: lax.all_gather(a, axis), part)  53 us
    while x128, local copies, waits for them, and re-layouts  19 us
    all_to_all x1, waiting for transfers between devices, copy_for_each(): lax.all_to_all(jnp.broadcast_to(x[None], (count, *x.shape)), axis, 0, 0,...  17.7 us
  transfers between devices with their start and end apart: 3, of which 2 were waited for; matrix products, arithmetic and copies ran while one was open for 5% of the time, Pallas kernels for 0%

commit v1 on v0

--- a/solution.py
+++ b/solution.py
@@ -202,7 +202,8 @@
     carried_in = entering((total, local), "seq", chain_step, identity)[1]
     prefix_out = emit(prefix_x, prefix_b, prefix_c, cum, skip_local, carried_in)
     beyond = entering_2(total, "seq", elementwise_product, jnp.ones_like(total))
-    final = lax.psum(beyond[:, None, None] * local, "seq")
+    apply_roots = lambda t0, mesh_dim: jnp.sum(lax.all_gather(t0, mesh_dim), 0)
+    final = apply_roots(beyond[:, None, None] * local, "seq")
     heads_final = gather_directly(final, "rep", 0)
     cand_heads = cand_decay.shape[2]
     cand_skip = lax.dynamic_slice_in_dim(

time: 710 us -> 1080 us (1.52)
  waiting for transfers between devices: 269 us -> 757 us
  blocking collectives: 191 us -> 57.5 us
  other arithmetic: 106 us -> 117 us
    all_gather x0 -> x1, waiting for transfers between devices: none -> 361 us  [on_device(): apply_roots = lambda t0, mesh_dim: jnp.sum(lax.all_gather(t0, mesh_dim), 0)]
    psum x1 -> x0, blocking collectives: 134 us -> none  [on_device(): final = lax.psum(beyond[:, None, None] * local, 'seq')]
    all_gather x1, waiting for transfers between devices: 251 us -> 361 us  [entering(): gathered = jax.tree.map(lambda a: lax.all_gather(a, axis), part)]
    all_gather x1, waiting for transfers between devices: 0.01 us -> 17.4 us  [sent_together(): result = lax.all_gather(both, axis, axis=dim, tiled=True)]
    reduce_sum x0 -> x1, other arithmetic: none -> 12 us  [on_device(): apply_roots = lambda t0, mesh_dim: jnp.sum(lax.all_gather(t0, mesh_dim), 0)]
  transfers between devices with their start and end apart: 3 -> 4, of which waited for: 2 -> 4; matrix products, arithmetic and copies ran while one was open for 5% -> 4% of each run, Pallas kernels for 0% -> 0%
where the time goes in v1:
time: 1080 us; the launch traced here: 1070 us
  waiting for transfers between devices  757 us (70%)
  other arithmetic  117 us (11%)
  local copies, waits for them, and re-layouts  99.1 us (9%)
  blocking collectives  57.5 us (5%)
  between operations  14.8 us (1%)
  matrix products  13.8 us (1%)
    all_gather x1, waiting for transfers between devices, entering(): gathered = jax.tree.map(lambda a: lax.all_gather(a, axis), part)  361 us
    all_gather x1, waiting for transfers between devices, on_device(): apply_roots = lambda t0, mesh_dim: jnp.sum(lax.all_gather(t0, mesh_dim), 0)  361 us
    add x31, other arithmetic, chain_step(): later[0][:, None, None] * earlier[1] + later[1]  99.7 us
    dynamic_slice x62, local copies, waits for them, and re-layouts, one(): lax.dynamic_index_in_dim(a, hop, 0, False)  59.4 us
    all_gather x1, blocking collectives, entering(): gathered = jax.tree.map(lambda a: lax.all_gather(a, axis), part)  52.9 us
  transfers between devices with their start and end apart: 4, of which 4 were waited for; matrix products, arithmetic and copies ran while one was open for 4% of the time, Pallas kernels for 0%

profile of v1, /device:TPU:2016, one launch (start us, length us, event | category | flops | bytes accessed | tf_op | source)
XLA Modules:
  0.0 1074.3 jit_solution(11174128698635868656)
XLA Ops:
  10.3 5.2 all-to-all-start
  16.9 17.8 %all-to-all-done = f32[32,1,16]{2,1,0:T(1,128)S(1)} async-done(((f32[32,1,16]{2,1,0:T(1,128)}), f32[32,1,16]{2,1,0:T(1,128)S(1)}, u32[]{:S(2)}, u32[]{:S(2)}) %all-to-all-start) | async-done | bytes 2080 | tf_op jit(solution)/shard_map/all_to_all | solution.py:26
  41.5 13.2 %while.56 = (s32[]{:T(128)}, f32[8,32,4,64]{3,1,2,0:T(8,128)S(1)}, bf16[8,32,4,64]{3,2,0,1:T(4,128)(2,1)S(1)}, f32[8,4,32]{2,1,0:T(4,128)S(1)}, s32[8]{0:T(128)S...) while((s32[]{:T(128)}, f32[8,32,4,64]{3,1,2,0:T(8,128)S(1)}, ...), condition=%wide.region_7.8_spmd.clone.clone, body=%wide.region_6.7_spmd.clone.clone.sunk | while | flops 549909 | bytes 166245 | solution.py:108
  56.1 52.9 %all-gather = f32[32,1,16]{2,1,0:T(1,128)S(1)} all-gather(f32[1,1,16]{2,1,0:T(1,128)S(1)} %get-tuple-element.433), channel_id=1, replica_groups=mesh['groups'=2,'seq'=32,'head'=4,'rep'=2] {'seq'}, dimensions={0}, use_global_device_ids=true | all-gather | bytes 2112 | tf_op jit(solution)/shard_map/all_gather | solution.py:13
  109.2 3.9 while.55
  113.1 17.4 %all-gather.9.cloned.1.call-done = bf16[4096,2,128]{2,0,1:T(8,128)(2,1)} async-done(((bf16[128,2,128]{2,0,1:T(8,128)(2,1)}), bf16[4096,2,128]{2,0,1:T(8,128)(2,1)}) %all-gather.9.cloned.1.call-update) | async-done | bytes 2097168 | tf_op jit(solution)/shard_map/all_gather | solution.py:62
  132.1 9.7 while.57
  143.2 360.5 %all-gather.7.cloned.1.call-done = f32[32,16,256,64]{2,3,1,0:T(8,128)} async-done(((f32[1,16,256,64]{2,3,1,0:T(8,128)}), f32[32,16,256,64]{2,3,1,0:T(8,128)}) %all-gather.7.cloned.1.call-update) | async-done | bytes 33554448 | tf_op jit(solution)/shard_map/all_gather | solution.py:205
  503.7 12.0 %reduce_sum.38 = bf16[16,256,64]{1,2,0:T(8,128)(2,1)S(1)} reduce(f32[32,16,256,64]{2,3,1,0:T(8,128)} %all-gather.7.cloned.1.call-done, f32[]{:T(128)} %constant.160.clone.1), dimensions={0}, to_apply=%region_8.9 | reduce | flops 8126464 | bytes 34078724 | tf_op jit(solution)/shard_map/reduce_sum | solution.py:205
  515.9 4.6 all_to_all.14
  522.2 360.8 %all-gather.5.cloned.1.call-done = f32[32,16,256,64]{2,3,1,0:T(8,128)} async-done(((f32[1,16,256,64]{2,3,1,0:T(8,128)}), f32[32,16,256,64]{2,3,1,0:T(8,128)}) %all-gather.5.cloned.1.call-update) | async-done | bytes 33554448 | tf_op jit(solution)/shard_map/all_gather | solution.py:13
  884.6 179.1 %while.54 = (s32[]{:T(128)}, f32[16,256,64]{2,1,0:T(8,128)}, s32[]{:T(128)}, f32[32,16]{1,0:T(8,128)S(1)}, f32[32,16,256,64]{2,3,1,0:T(8,128)}, /*index=5*/s32[]{:T(128)}, s32[]{:T(128)}, s32[]{:T(128)}) while((s32[]{:T(128)}, f32[16,256,64]{2,1,0:T(8,128)}, s32[]{:T(128)}, f32[32,16]{1,0:T(8,128)S(1)}, f32[32,16,256,64]{2,3,1,0:T(8,128)}, ...), condition=%wide.region_4.5_spmd, body=%wide.region_3.4_spmd.sunk | while | flops 524293 | bytes 7356799 | solution.py:21
  887.1 3.2 bitcast_add_fusion.4
  892.9 3.2 bitcast_add_fusion.4
  898.7 3.2 bitcast_add_fusion.4
  904.5 3.2 bitcast_add_fusion.4
  910.2 3.2 bitcast_add_fusion.4
  916.0 3.2 bitcast_add_fusion.4
  921.8 3.2 bitcast_add_fusion.4
  927.6 3.2 bitcast_add_fusion.4
  933.3 3.2 bitcast_add_fusion.4
  939.1 3.2 bitcast_add_fusion.4
  944.9 3.2 bitcast_add_fusion.4
  950.7 3.2 bitcast_add_fusion.4
  956.5 3.2 bitcast_add_fusion.4
  962.2 3.2 bitcast_add_fusion.4
  968.0 3.2 bitcast_add_fusion.4
  973.8 3.2 bitcast_add_fusion.4
  979.6 3.2 bitcast_add_fusion.4
  985.3 3.2 bitcast_add_fusion.4
  1002.7 3.2 bitcast_add_fusion.4
  1054.7 3.2 bitcast_add_fusion.4
  (435 shorter events, 154.4 us)
Async XLA Ops:
  7.2 27.8 %copy-start = (bf16[128,1,256]{2,0,1:T(8,128)(2,1)S(1)}, bf16[128,1,256]{2,0,1:T(8,128)(2,1)}, u32[]{:S(2)}) copy-start(bf16[128,1,256]{2,0,1:T(8,128)(2,1)} %param.24) | copy-start | bytes 196612
  7.2 123.2 %all-gather.9.cloned.1.call-start = ((), (), s32[]{:S(2)}) async-start(), calls=%async_computation.4 | async-start | bytes 2162688 | tf_op jit(solution)/shard_map/all_gather | solution.py:62
  10.3 24.3 %all-to-all-start = ((f32[32,1,16]{2,1,0:T(1,128)}), f32[32,1,16]{2,1,0:T(1,128)S(1)}, u32[]{:S(2)}, u32[]{:S(2)}) async-start(f32[32,1,16]{2,1,0:T(1,128)} %broadcast_in_dim.151), calls=%async_computation | async-start | bytes 32768 | tf_op jit(solution)/shard_map/all_to_all | solution.py:26
  15.5 488.2 %all-gather.7.cloned.1.call-start = ((), (), s32[]{:S(2)}) async-start(), calls=%async_computation.3 | async-start | bytes 34603008 | tf_op jit(solution)/shard_map/all_gather | solution.py:205
  35.0 3.3 copy-start.20
  35.0 4.3 copy-start.13
  35.0 4.5 copy-start.8
  35.0 4.6 copy-start.16
  36.6 3.4 copy-start.6
  36.7 4.6 copy-start.10
  36.7 4.6 copy-start.11
  36.7 846.3 %all-gather.5.cloned.1.call-start = ((), (), s32[]{:S(2)}) async-start(), calls=%async_computation.2 | async-start | bytes 34603008 | tf_op jit(solution)/shard_map/all_gather | solution.py:13
  41.3 67.8 %copy-start.9 = (bf16[128,1,256]{2,0,1:T(8,128)(2,1)S(1)}, bf16[128,1,256]{2,0,1:T(8,128)(2,1)}, u32[]{:S(2)}) copy-start(bf16[128,1,256]{2,0,1:T(8,128)(2,1)} %param.25) | copy-start | bytes 196612
  109.1 33.3 %copy-start.17 = (pred[32]{0:T(512)(128)(4,1)}, pred[32]{0:T(512)(128)(4,1)S(1)}, u32[]{:S(2)}) copy-start(pred[32]{0:T(512)(128)(4,1)S(1)} %iota_compare_fusion.4) | copy-start | bytes 100
  132.1 10.0 copy-start.19
  887.1 3.2 copy-start.15
  892.9 3.2 copy-start.15
  898.7 3.2 copy-start.15
  904.5 3.2 copy-start.15
  916.0 3.2 copy-start.15
  921.8 3.2 copy-start.15
  927.6 3.2 copy-start.15
  933.3 3.2 copy-start.15
  939.1 3.2 copy-start.15
  944.9 3.2 copy-start.15
  950.7 3.2 copy-start.15
  1063.7 3.3 copy-start.2
  1063.7 3.3 copy-start.3
  1063.7 3.3 copy-start.4
  1063.7 3.3 copy-start.7
  1063.7 3.3 copy-start.18
  1063.7 4.1 copy-start.1
  (53 other events, 87.9 us)
Sparse Core Ops, SparseCore 0:
  10.7 119.6 all-gather.8
  132.5 371.1 all-gather.6
  505.8 377.1 all-gather.4
